TPU v7x, 32 devices: a whole 2x2x4 slice. The times are simulated.
32 devices in a mesh: tm: 8 (over z, y), space: 4 (over x, core).
Axes of the slice: x: 2, y: 2, z: 4, core: 2. Of those that a mesh axis runs over, the one named last changes fastest.
Arguments:
- c_points: float32 [8, 64, 32, 128], P('tm', 'space'), may hold values from -15 to 15
- corrections: float32 [8, 64, 32, 128], P('tm', 'space'), may hold values from -3 to 3
- conductivity: float32 [64, 32, 128], P('space'), may hold values from 0.2 to 5
- forcing: float32 [64, 32, 128], P('space'), may hold values from -6 to 6
Outputs:
- f_states: float32 [8, 2, 64, 32, 128], P('tm', None, 'space')
All inputs are finite; a program needn't handle non-finite values.
Results may differ from a plain program's by a relative error of at most 0.0002.
Values sent between devices are 32-bit elements; how exact they have to be, the bound alone decides.
A program may use at most 64 MiB of HBM per device.

v0:
```python
import jax
import jax.numpy as jnp
from jax import lax
from jax.sharding import PartitionSpec as P

ITERS = 6
STEPS = 2


step_rate = 4.0
source_weight = 0.25


def extended(cells, sides, width):
    for axis, dim in sides:
        count = lax.axis_size(axis)
        ends = count - 1
        head = lax.slice_in_dim(cells, 0, width, axis=dim)
        tail = lax.slice_in_dim(cells, cells.shape[dim] - width, cells.shape[dim], axis=dim)
        cells = jnp.concatenate(
            [
                lax.ppermute(tail, axis, [(i, (i + 1) % count) for i in range(ends)]),
                cells,
                lax.ppermute(head, axis, [((i + 1) % count, i) for i in range(ends)]),
            ],
            axis=dim,
        )
    return cells


def from_behind(array, axis, by):
    devices = lax.axis_size(axis)
    pairs = [(i, i + by) for i in range(devices) if 0 <= i + by < devices]
    return lax.ppermute(array, axis, pairs)


def neighbours(padded):
    return (
        padded[2:, 1:-1, 1:-1],
        padded[:-2, 1:-1, 1:-1],
        padded[1:-1, 2:, 1:-1],
        padded[1:-1, :-2, 1:-1],
        padded[1:-1, 1:-1, 2:],
        padded[1:-1, 1:-1, :-2],
    )


def faces_of(padded_conductivity):
    centre = padded_conductivity[1:-1, 1:-1, 1:-1]
    return tuple((0.5 * (centre + beside) for beside in neighbours(padded_conductivity)))


def apply_operator(grid_field, padded, face_weights):
    flux_sum = jnp.zeros_like(grid_field)
    for face_weight, beside in zip(face_weights, neighbours(padded)):
        flux_sum = flux_sum + face_weight * (grid_field - beside)
    return grid_field + step_rate * flux_sum


def pair_sums(residual, applied):
    return lax.psum((jnp.sum(residual * residual), jnp.sum(residual * applied)), "space")


def body(c_points, corrections, conductivity, forcing):
    rim_conductivity = extended(conductivity, (("space", 0),), 1)
    face_weights = faces_of(jnp.pad(rim_conductivity, ((0, 0), (1, 1), (1, 1))))

    def operate(grid_field):
        with_planes = extended(grid_field, (("space", 0),), 1)
        padded = jnp.pad(with_planes, ((0, 0), (1, 1), (1, 1)))
        return apply_operator(grid_field, padded, face_weights)

    own_point = c_points[0]
    own_fix = corrections[0]
    prior_fix = from_behind(own_fix, "tm", 1)
    current = own_point + prior_fix
    current_image = operate(current)
    sections = []
    for section in range(STEPS):
        right_side = current + source_weight * forcing
        if section > 0:
            current_image = operate(current)
        residual = right_side - current_image
        solution = current
        applied = operate(residual)
        norm_now, product = pair_sums(residual, applied)
        step_length = norm_now / product
        direction = residual
        along_dir = applied
        for sweep in range(ITERS):
            solution = solution + step_length * direction
            if sweep + 1 < ITERS:
                residual = residual - step_length * along_dir
                applied = operate(residual)
                norm_next, product = pair_sums(residual, applied)
                beta_ratio = norm_next / norm_now
                step_length = norm_next / (product - beta_ratio * norm_next / step_length)
                direction = residual + beta_ratio * direction
                along_dir = applied + beta_ratio * along_dir
                norm_now = norm_next
        sections.append(solution)
        current = solution
    return jnp.stack(sections)[None]


def solution(mesh):
    in_specs = (
        P("tm", "space", None, None),
        P("tm", "space", None, None),
        P("space", None, None),
        P("space", None, None),
    )
    out_specs = P("tm", None, "space", None, None)
    return jax.shard_map(body, mesh=mesh, in_specs=in_specs, out_specs=out_specs, check_vma=False)
```

profile of v0, /device:TPU:0, one launch (start us, length us, event | category | flops | bytes accessed | tf_op | source)
XLA Modules:
  0.0 275.3 jit_solution(7316067499902475221)
XLA Ops:
  0.0 4.9 %collective-permute-start = (f32[16,32,128]{2,1,0:T(8,128)}, f32[16,32,128]{2,1,0:T(8,128)S(1)}, u32[]{:S(2)}, u32[]{:S(2)}) collective-permute-start(f32[16,32,128]{2,1,0:T(8,128)} %bitcast.9), channel_id=1, source_target_pairs={{0,4},{4,8},{8,12},{12,16},{16,20},{20,24},{24,28},{1,5},{5,9},{9,... | collective-permute-start | bytes 786440 | tf_op jit(solution)/shard_map/ppermute | solution.py:34
  5.7 1.4 collective-permute-start.3
  7.1 1.4 collective-permute-start.1
  8.6 2.2 collective-permute-done
  11.8 2.4 collective-permute-start.4
  15.8 2.7 collective-permute-done.2
  19.3 4.4 %collective-permute-start.6 = (f32[1,32,128]{2,1,0:T(8,128)S(1)}, f32[1,32,128]{2,1,0:T(8,128)S(1)}, u32[]{:S(2)}, u32[]{:S(2)}) collective-permute-start(f32[1,32,128]{2,1,0:T(8,128)S(1)} %get-tuple-element.96), channel_id=1, source_target_pairs={{0,1},{1,2},{2,3},{4,5},{5,6},{6,7},{8,9},{9,10},{10,11},{12,13},{... | collective-permute-start | bytes 49160 | tf_op jit(solution)/shard_map/ppermute | solution.py:22
  25.0 1.8 collective-permute-done.5
  28.1 8.3 %all-reduce.26 = (f32[]{:T(128)}, f32[]{:T(128)}) all-reduce(f32[]{:T(128)} %get-tuple-element.28, f32[]{:T(128)} %get-tuple-element.27), channel_id=1, replica_groups=mesh['tm'=8,'space'=4] {'space'}, use_global_device_ids=true, to_apply=%region_1.2 | all-reduce | flops 2 | bytes 16 | tf_op jit(solution)/shard_map/psum | solution.py:61
  37.7 1.4 collective-permute-start.8
  40.4 3.6 %collective-permute-done.7 = f32[1,32,128]{2,1,0:T(8,128)S(1)} collective-permute-done((f32[1,32,128]{2,1,0:T(8,128)S(1)}, f32[1,32,128]{2,1,0:T(8,128)S(1)}, u32[]{:S(2)}, u32[]{:S(2)}) %collective-permute-start.7) | collective-permute-done | bytes 16416 | tf_op jit(solution)/shard_map/ppermute | solution.py:24
  45.2 8.8 %all-reduce.25 = (f32[]{:T(128)}, f32[]{:T(128)}) all-reduce(f32[]{:T(128)} %get-tuple-element.26, f32[]{:T(128)} %get-tuple-element.25), channel_id=1, replica_groups=mesh['tm'=8,'space'=4] {'space'}, use_global_device_ids=true, to_apply=%region_5.6 | all-reduce | flops 2 | bytes 16 | tf_op jit(solution)/shard_map/psum | solution.py:61
  58.6 1.4 collective-permute-start.10
  61.3 3.6 %collective-permute-done.9 = f32[1,32,128]{2,1,0:T(8,128)S(1)} collective-permute-done((f32[1,32,128]{2,1,0:T(8,128)S(1)}, f32[1,32,128]{2,1,0:T(8,128)S(1)}, u32[]{:S(2)}, u32[]{:S(2)}) %collective-permute-start.9) | collective-permute-done | bytes 16416 | tf_op jit(solution)/shard_map/ppermute | solution.py:24
  65.1 1.7 multiply_reduce_fusion.16
  66.9 8.8 %all-reduce.24 = (f32[]{:T(128)}, f32[]{:T(128)}) all-reduce(f32[]{:T(128)} %get-tuple-element.24, f32[]{:T(128)} %get-tuple-element.23), channel_id=1, replica_groups=mesh['tm'=8,'space'=4] {'space'}, use_global_device_ids=true, to_apply=%region_9.10 | all-reduce | flops 2 | bytes 16 | tf_op jit(solution)/shard_map/psum | solution.py:61
  80.6 1.4 collective-permute-start.12
  83.3 3.6 %collective-permute-done.11 = f32[1,32,128]{2,1,0:T(8,128)S(1)} collective-permute-done((f32[1,32,128]{2,1,0:T(8,128)S(1)}, f32[1,32,128]{2,1,0:T(8,128)S(1)}, u32[]{:S(2)}, u32[]{:S(2)}) %collective-permute-start.11) | collective-permute-done | bytes 16416 | tf_op jit(solution)/shard_map/ppermute | solution.py:24
  88.1 8.8 %all-reduce.23 = (f32[]{:T(128)}, f32[]{:T(128)}) all-reduce(f32[]{:T(128)} %get-tuple-element.22, f32[]{:T(128)} %get-tuple-element.21), channel_id=1, replica_groups=mesh['tm'=8,'space'=4] {'space'}, use_global_device_ids=true, to_apply=%region_13.14 | all-reduce | flops 2 | bytes 16 | tf_op jit(solution)/shard_map/psum | solution.py:61
  100.8 1.4 collective-permute-start.14
  103.5 3.6 %collective-permute-done.13 = f32[1,32,128]{2,1,0:T(8,128)S(1)} collective-permute-done((f32[1,32,128]{2,1,0:T(8,128)S(1)}, f32[1,32,128]{2,1,0:T(8,128)S(1)}, u32[]{:S(2)}, u32[]{:S(2)}) %collective-permute-start.13) | collective-permute-done | bytes 16416 | tf_op jit(solution)/shard_map/ppermute | solution.py:24
  107.3 1.7 multiply_reduce_fusion.12
  109.1 8.8 %all-reduce.22 = (f32[]{:T(128)}, f32[]{:T(128)}) all-reduce(f32[]{:T(128)} %get-tuple-element.20, f32[]{:T(128)} %get-tuple-element.19), channel_id=1, replica_groups=mesh['tm'=8,'space'=4] {'space'}, use_global_device_ids=true, to_apply=%region_17.18 | all-reduce | flops 2 | bytes 16 | tf_op jit(solution)/shard_map/psum | solution.py:61
  122.8 1.4 collective-permute-start.16
  125.5 3.6 %collective-permute-done.15 = f32[1,32,128]{2,1,0:T(8,128)S(1)} collective-permute-done((f32[1,32,128]{2,1,0:T(8,128)S(1)}, f32[1,32,128]{2,1,0:T(8,128)S(1)}, u32[]{:S(2)}, u32[]{:S(2)}) %collective-permute-start.15) | collective-permute-done | bytes 16416 | tf_op jit(solution)/shard_map/ppermute | solution.py:24
  130.3 8.8 %all-reduce.21 = (f32[]{:T(128)}, f32[]{:T(128)}) all-reduce(f32[]{:T(128)} %get-tuple-element.18, f32[]{:T(128)} %get-tuple-element.17), channel_id=1, replica_groups=mesh['tm'=8,'space'=4] {'space'}, use_global_device_ids=true, to_apply=%region_21.22 | all-reduce | flops 2 | bytes 16 | tf_op jit(solution)/shard_map/psum | solution.py:61
  143.4 1.4 collective-permute-start.18
  144.8 1.4 collective-permute-start.17
  146.2 3.6 %collective-permute-done.17 = f32[1,32,128]{2,1,0:T(8,128)S(1)} collective-permute-done((f32[1,32,128]{2,1,0:T(8,128)S(1)}, f32[1,32,128]{2,1,0:T(8,128)S(1)}, u32[]{:S(2)}, u32[]{:S(2)}) %collective-permute-start.17) | collective-permute-done | bytes 16416 | tf_op jit(solution)/shard_map/ppermute | solution.py:24
  150.4 4.4 %collective-permute-start.20 = (f32[1,32,128]{2,1,0:T(8,128)S(1)}, f32[1,32,128]{2,1,0:T(8,128)S(1)}, u32[]{:S(2)}, u32[]{:S(2)}) collective-permute-start(f32[1,32,128]{2,1,0:T(8,128)S(1)} %get-tuple-element.82), channel_id=1, source_target_pairs={{0,1},{1,2},{2,3},{4,5},{5,6},{6,7},{8,9},{9,10},{10,11},{12,13},{... | collective-permute-start | bytes 49160 | tf_op jit(solution)/shard_map/ppermute | solution.py:22
  156.1 1.8 collective-permute-done.19
  159.2 8.3 %all-reduce.20 = (f32[]{:T(128)}, f32[]{:T(128)}) all-reduce(f32[]{:T(128)} %get-tuple-element.16, f32[]{:T(128)} %get-tuple-element.15), channel_id=1, replica_groups=mesh['tm'=8,'space'=4] {'space'}, use_global_device_ids=true, to_apply=%region_25.26 | all-reduce | flops 2 | bytes 16 | tf_op jit(solution)/shard_map/psum | solution.py:61
  168.8 1.4 collective-permute-start.22
  171.5 3.6 %collective-permute-done.21 = f32[1,32,128]{2,1,0:T(8,128)S(1)} collective-permute-done((f32[1,32,128]{2,1,0:T(8,128)S(1)}, f32[1,32,128]{2,1,0:T(8,128)S(1)}, u32[]{:S(2)}, u32[]{:S(2)}) %collective-permute-start.21) | collective-permute-done | bytes 16416 | tf_op jit(solution)/shard_map/ppermute | solution.py:24
  176.3 8.8 %all-reduce.19 = (f32[]{:T(128)}, f32[]{:T(128)}) all-reduce(f32[]{:T(128)} %get-tuple-element.14, f32[]{:T(128)} %get-tuple-element.13), channel_id=1, replica_groups=mesh['tm'=8,'space'=4] {'space'}, use_global_device_ids=true, to_apply=%region_29.30 | all-reduce | flops 2 | bytes 16 | tf_op jit(solution)/shard_map/psum | solution.py:61
  189.8 1.4 collective-permute-start.24
  192.5 3.6 %collective-permute-done.23 = f32[1,32,128]{2,1,0:T(8,128)S(1)} collective-permute-done((f32[1,32,128]{2,1,0:T(8,128)S(1)}, f32[1,32,128]{2,1,0:T(8,128)S(1)}, u32[]{:S(2)}, u32[]{:S(2)}) %collective-permute-start.23) | collective-permute-done | bytes 16416 | tf_op jit(solution)/shard_map/ppermute | solution.py:24
  196.3 1.7 multiply_reduce_fusion.5
  198.0 8.8 %all-reduce.18 = (f32[]{:T(128)}, f32[]{:T(128)}) all-reduce(f32[]{:T(128)} %get-tuple-element.12, f32[]{:T(128)} %get-tuple-element.11), channel_id=1, replica_groups=mesh['tm'=8,'space'=4] {'space'}, use_global_device_ids=true, to_apply=%region_33.34 | all-reduce | flops 2 | bytes 16 | tf_op jit(solution)/shard_map/psum | solution.py:61
  211.8 1.4 collective-permute-start.26
  213.2 1.5 collective-permute-start.25
  214.6 3.4 %collective-permute-done.25 = f32[1,32,128]{2,1,0:T(8,128)S(1)} collective-permute-done((f32[1,32,128]{2,1,0:T(8,128)S(1)}, f32[1,32,128]{2,1,0:T(8,128)S(1)}, u32[]{:S(2)}, u32[]{:S(2)}) %collective-permute-start.25) | collective-permute-done | bytes 16416 | tf_op jit(solution)/shard_map/ppermute | solution.py:24
  219.2 8.8 %all-reduce.17 = (f32[]{:T(128)}, f32[]{:T(128)}) all-reduce(f32[]{:T(128)} %get-tuple-element.10, f32[]{:T(128)} %get-tuple-element.9), channel_id=1, replica_groups=mesh['tm'=8,'space'=4] {'space'}, use_global_device_ids=true, to_apply=%region_37.38 | all-reduce | flops 2 | bytes 16 | tf_op jit(solution)/shard_map/psum | solution.py:61
  234.7 3.6 %collective-permute-done.27 = f32[1,32,128]{2,1,0:T(8,128)S(1)} collective-permute-done((f32[1,32,128]{2,1,0:T(8,128)S(1)}, f32[1,32,128]{2,1,0:T(8,128)S(1)}, u32[]{:S(2)}, u32[]{:S(2)}) %collective-permute-start.27) | collective-permute-done | bytes 16416 | tf_op jit(solution)/shard_map/ppermute | solution.py:24
  238.5 1.7 multiply_reduce_fusion.1
  240.2 8.8 %all-reduce.16 = (f32[]{:T(128)}, f32[]{:T(128)}) all-reduce(f32[]{:T(128)} %get-tuple-element.8, f32[]{:T(128)} %get-tuple-element.7), channel_id=1, replica_groups=mesh['tm'=8,'space'=4] {'space'}, use_global_device_ids=true, to_apply=%region_41.42 | all-reduce | flops 2 | bytes 16 | tf_op jit(solution)/shard_map/psum | solution.py:61
  256.6 3.6 %collective-permute-done.29 = f32[1,32,128]{2,1,0:T(8,128)S(1)} collective-permute-done((f32[1,32,128]{2,1,0:T(8,128)S(1)}, f32[1,32,128]{2,1,0:T(8,128)S(1)}, u32[]{:S(2)}, u32[]{:S(2)}) %collective-permute-start.29) | collective-permute-done | bytes 16416 | tf_op jit(solution)/shard_map/ppermute | solution.py:24
  261.4 8.8 %all-reduce.15 = (f32[]{:T(128)}, f32[]{:T(128)}) all-reduce(f32[]{:T(128)} %get-tuple-element.6, f32[]{:T(128)} %get-tuple-element.5), channel_id=1, replica_groups=mesh['tm'=8,'space'=4] {'space'}, use_global_device_ids=true, to_apply=%region_45.46 | all-reduce | flops 2 | bytes 16 | tf_op jit(solution)/shard_map/psum | solution.py:61
  (94 shorter events, 38.9 us)
Async XLA Ops:
  0.0 10.8 %collective-permute-start = (f32[16,32,128]{2,1,0:T(8,128)}, f32[16,32,128]{2,1,0:T(8,128)S(1)}, u32[]{:S(2)}, u32[]{:S(2)}) collective-permute-start(f32[16,32,128]{2,1,0:T(8,128)} %bitcast.9), channel_id=1, source_target_pairs={{0,4},{4,8},{8,12},{12,16},{16,20},{20,24},{24,28},{1,5},{5,9},{9,... | collective-permute-start | bytes 786440 | tf_op jit(solution)/shard_map/ppermute | solution.py:34
  5.7 9.8 %collective-permute-start.3 = (f32[1,32,128]{2,1,0:T(8,128)S(1)}, f32[1,32,128]{2,1,0:T(8,128)S(1)}, u32[]{:S(2)}, u32[]{:S(2)}) collective-permute-start(f32[1,32,128]{2,1,0:T(8,128)S(1)} %get-tuple-element.98), channel_id=1, source_target_pairs={{0,1},{1,2},{2,3},{4,5},{5,6},{6,7},{8,9},{9,10},{10,11},{12,13},{... | collective-permute-start | bytes 49160 | tf_op jit(solution)/shard_map/ppermute | solution.py:22
  7.1 8.4 %copy-start = (f32[16,32,128]{2,1,0:T(8,128)S(1)}, f32[16,32,128]{2,1,0:T(8,128)}, u32[]{:S(2)}) copy-start(f32[16,32,128]{2,1,0:T(8,128)} %param.6) | copy-start | bytes 786436
  7.1 8.4 %collective-permute-start.1 = (f32[1,32,128]{2,1,0:T(8,128)S(1)}, f32[1,32,128]{2,1,0:T(8,128)S(1)}, u32[]{:S(2)}, u32[]{:S(2)}) collective-permute-start(f32[1,32,128]{2,1,0:T(8,128)S(1)} %get-tuple-element.99), channel_id=1, source_target_pairs={{1,0},{2,1},{3,2},{5,4},{6,5},{7,6},{9,8},{10,9},{11,10},{13,12},{... | collective-permute-start | bytes 49160 | tf_op jit(solution)/shard_map/ppermute | solution.py:24
  11.8 4.0 %collective-permute-start.4 = (f32[1,32,128]{2,1,0:T(8,128)S(1)}, f32[1,32,128]{2,1,0:T(8,128)S(1)}, u32[]{:S(2)}, u32[]{:S(2)}) collective-permute-start(f32[1,32,128]{2,1,0:T(8,128)S(1)} %get-tuple-element.100), channel_id=1, source_target_pairs={{0,1},{1,2},{2,3},{4,5},{5,6},{6,7},{8,9},{9,10},{10,11},{12,13},{... | collective-permute-start | bytes 49160 | tf_op jit(solution)/shard_map/ppermute | solution.py:22
  14.2 4.3 %collective-permute-start.2 = (f32[1,32,128]{2,1,0:T(8,128)S(1)}, f32[1,32,128]{2,1,0:T(8,128)S(1)}, u32[]{:S(2)}, u32[]{:S(2)}) collective-permute-start(f32[1,32,128]{2,1,0:T(8,128)S(1)} %get-tuple-element.101), channel_id=1, source_target_pairs={{1,0},{2,1},{3,2},{5,4},{6,5},{7,6},{9,8},{10,9},{11,10},{13,12},{... | collective-permute-start | bytes 49160 | tf_op jit(solution)/shard_map/ppermute | solution.py:24
  15.8 3.0 %copy-start.3 = (f32[16,32,128]{2,1,0:T(8,128)S(1)}, f32[16,32,128]{2,1,0:T(8,128)}, u32[]{:S(2)}) copy-start(f32[16,32,128]{2,1,0:T(8,128)} %param.7) | copy-start | bytes 786436
  19.3 5.7 %collective-permute-start.6 = (f32[1,32,128]{2,1,0:T(8,128)S(1)}, f32[1,32,128]{2,1,0:T(8,128)S(1)}, u32[]{:S(2)}, u32[]{:S(2)}) collective-permute-start(f32[1,32,128]{2,1,0:T(8,128)S(1)} %get-tuple-element.96), channel_id=1, source_target_pairs={{0,1},{1,2},{2,3},{4,5},{5,6},{6,7},{8,9},{9,10},{10,11},{12,13},{... | collective-permute-start | bytes 49160 | tf_op jit(solution)/shard_map/ppermute | solution.py:22
  23.7 3.1 %collective-permute-start.5 = (f32[1,32,128]{2,1,0:T(8,128)S(1)}, f32[1,32,128]{2,1,0:T(8,128)S(1)}, u32[]{:S(2)}, u32[]{:S(2)}) collective-permute-start(f32[1,32,128]{2,1,0:T(8,128)S(1)} %get-tuple-element.97), channel_id=1, source_target_pairs={{1,0},{2,1},{3,2},{5,4},{6,5},{7,6},{9,8},{10,9},{11,10},{13,12},{... | collective-permute-start | bytes 49160 | tf_op jit(solution)/shard_map/ppermute | solution.py:24
  37.7 2.7 collective-permute-start.8
  39.1 4.9 %collective-permute-start.7 = (f32[1,32,128]{2,1,0:T(8,128)S(1)}, f32[1,32,128]{2,1,0:T(8,128)S(1)}, u32[]{:S(2)}, u32[]{:S(2)}) collective-permute-start(f32[1,32,128]{2,1,0:T(8,128)S(1)} %get-tuple-element.95), channel_id=1, source_target_pairs={{1,0},{2,1},{3,2},{5,4},{6,5},{7,6},{9,8},{10,9},{11,10},{13,12},{... | collective-permute-start | bytes 49160 | tf_op jit(solution)/shard_map/ppermute | solution.py:24
  58.6 2.7 collective-permute-start.10
  60.0 4.9 %collective-permute-start.9 = (f32[1,32,128]{2,1,0:T(8,128)S(1)}, f32[1,32,128]{2,1,0:T(8,128)S(1)}, u32[]{:S(2)}, u32[]{:S(2)}) collective-permute-start(f32[1,32,128]{2,1,0:T(8,128)S(1)} %get-tuple-element.93), channel_id=1, source_target_pairs={{1,0},{2,1},{3,2},{5,4},{6,5},{7,6},{9,8},{10,9},{11,10},{13,12},{... | collective-permute-start | bytes 49160 | tf_op jit(solution)/shard_map/ppermute | solution.py:24
  80.6 2.7 collective-permute-start.12
  82.0 4.9 %collective-permute-start.11 = (f32[1,32,128]{2,1,0:T(8,128)S(1)}, f32[1,32,128]{2,1,0:T(8,128)S(1)}, u32[]{:S(2)}, u32[]{:S(2)}) collective-permute-start(f32[1,32,128]{2,1,0:T(8,128)S(1)} %get-tuple-element.91), channel_id=1, source_target_pairs={{1,0},{2,1},{3,2},{5,4},{6,5},{7,6},{9,8},{10,9},{11,10},{13,12},{... | collective-permute-start | bytes 49160 | tf_op jit(solution)/shard_map/ppermute | solution.py:24
  88.1 19.2 %copy-start.1 = (f32[16,32,128]{2,1,0:T(8,128)}, f32[16,32,128]{2,1,0:T(8,128)S(1)}, u32[]{:S(2)}) copy-start(f32[16,32,128]{2,1,0:T(8,128)S(1)} %get-tuple-element.61) | copy-start | bytes 786436
  100.8 2.7 collective-permute-start.14
  102.2 4.9 %collective-permute-start.13 = (f32[1,32,128]{2,1,0:T(8,128)S(1)}, f32[1,32,128]{2,1,0:T(8,128)S(1)}, u32[]{:S(2)}, u32[]{:S(2)}) collective-permute-start(f32[1,32,128]{2,1,0:T(8,128)S(1)} %get-tuple-element.89), channel_id=1, source_target_pairs={{1,0},{2,1},{3,2},{5,4},{6,5},{7,6},{9,8},{10,9},{11,10},{13,12},{... | collective-permute-start | bytes 49160 | tf_op jit(solution)/shard_map/ppermute | solution.py:24
  122.8 2.7 collective-permute-start.16
  124.2 4.9 %collective-permute-start.15 = (f32[1,32,128]{2,1,0:T(8,128)S(1)}, f32[1,32,128]{2,1,0:T(8,128)S(1)}, u32[]{:S(2)}, u32[]{:S(2)}) collective-permute-start(f32[1,32,128]{2,1,0:T(8,128)S(1)} %get-tuple-element.87), channel_id=1, source_target_pairs={{1,0},{2,1},{3,2},{5,4},{6,5},{7,6},{9,8},{10,9},{11,10},{13,12},{... | collective-permute-start | bytes 49160 | tf_op jit(solution)/shard_map/ppermute | solution.py:24
  143.4 2.8 %collective-permute-start.18 = (f32[1,32,128]{2,1,0:T(8,128)S(1)}, f32[1,32,128]{2,1,0:T(8,128)S(1)}, u32[]{:S(2)}, u32[]{:S(2)}) collective-permute-start(f32[1,32,128]{2,1,0:T(8,128)S(1)} %get-tuple-element.84), channel_id=1, source_target_pairs={{0,1},{1,2},{2,3},{4,5},{5,6},{6,7},{8,9},{9,10},{10,11},{12,13},{... | collective-permute-start | bytes 49160 | tf_op jit(solution)/shard_map/ppermute | solution.py:22
  144.8 5.3 %copy-start.4 = (f32[16,32,128]{2,1,0:T(8,128)S(1)}, f32[16,32,128]{2,1,0:T(8,128)}, u32[]{:S(2)}) copy-start(f32[16,32,128]{2,1,0:T(8,128)} %param.7) | copy-start | bytes 786436
  144.8 5.0 %collective-permute-start.17 = (f32[1,32,128]{2,1,0:T(8,128)S(1)}, f32[1,32,128]{2,1,0:T(8,128)S(1)}, u32[]{:S(2)}, u32[]{:S(2)}) collective-permute-start(f32[1,32,128]{2,1,0:T(8,128)S(1)} %get-tuple-element.85), channel_id=1, source_target_pairs={{1,0},{2,1},{3,2},{5,4},{6,5},{7,6},{9,8},{10,9},{11,10},{13,12},{... | collective-permute-start | bytes 49160 | tf_op jit(solution)/shard_map/ppermute | solution.py:24
  150.4 5.7 %collective-permute-start.20 = (f32[1,32,128]{2,1,0:T(8,128)S(1)}, f32[1,32,128]{2,1,0:T(8,128)S(1)}, u32[]{:S(2)}, u32[]{:S(2)}) collective-permute-start(f32[1,32,128]{2,1,0:T(8,128)S(1)} %get-tuple-element.82), channel_id=1, source_target_pairs={{0,1},{1,2},{2,3},{4,5},{5,6},{6,7},{8,9},{9,10},{10,11},{12,13},{... | collective-permute-start | bytes 49160 | tf_op jit(solution)/shard_map/ppermute | solution.py:22
  154.8 3.1 %collective-permute-start.19 = (f32[1,32,128]{2,1,0:T(8,128)S(1)}, f32[1,32,128]{2,1,0:T(8,128)S(1)}, u32[]{:S(2)}, u32[]{:S(2)}) collective-permute-start(f32[1,32,128]{2,1,0:T(8,128)S(1)} %get-tuple-element.83), channel_id=1, source_target_pairs={{1,0},{2,1},{3,2},{5,4},{6,5},{7,6},{9,8},{10,9},{11,10},{13,12},{... | collective-permute-start | bytes 49160 | tf_op jit(solution)/shard_map/ppermute | solution.py:24
  168.8 2.7 collective-permute-start.22
  170.2 4.9 %collective-permute-start.21 = (f32[1,32,128]{2,1,0:T(8,128)S(1)}, f32[1,32,128]{2,1,0:T(8,128)S(1)}, u32[]{:S(2)}, u32[]{:S(2)}) collective-permute-start(f32[1,32,128]{2,1,0:T(8,128)S(1)} %get-tuple-element.81), channel_id=1, source_target_pairs={{1,0},{2,1},{3,2},{5,4},{6,5},{7,6},{9,8},{10,9},{11,10},{13,12},{... | collective-permute-start | bytes 49160 | tf_op jit(solution)/shard_map/ppermute | solution.py:24
  189.8 2.7 collective-permute-start.24
  191.2 4.9 %collective-permute-start.23 = (f32[1,32,128]{2,1,0:T(8,128)S(1)}, f32[1,32,128]{2,1,0:T(8,128)S(1)}, u32[]{:S(2)}, u32[]{:S(2)}) collective-permute-start(f32[1,32,128]{2,1,0:T(8,128)S(1)} %get-tuple-element.79), channel_id=1, source_target_pairs={{1,0},{2,1},{3,2},{5,4},{6,5},{7,6},{9,8},{10,9},{11,10},{13,12},{... | collective-permute-start | bytes 49160 | tf_op jit(solution)/shard_map/ppermute | solution.py:24
  211.8 2.9 %collective-permute-start.26 = (f32[1,32,128]{2,1,0:T(8,128)S(1)}, f32[1,32,128]{2,1,0:T(8,128)S(1)}, u32[]{:S(2)}, u32[]{:S(2)}) collective-permute-start(f32[1,32,128]{2,1,0:T(8,128)S(1)} %get-tuple-element.76), channel_id=1, source_target_pairs={{0,1},{1,2},{2,3},{4,5},{5,6},{6,7},{8,9},{9,10},{10,11},{12,13},{... | collective-permute-start | bytes 49160 | tf_op jit(solution)/shard_map/ppermute | solution.py:22
  213.2 4.9 %collective-permute-start.25 = (f32[1,32,128]{2,1,0:T(8,128)S(1)}, f32[1,32,128]{2,1,0:T(8,128)S(1)}, u32[]{:S(2)}, u32[]{:S(2)}) collective-permute-start(f32[1,32,128]{2,1,0:T(8,128)S(1)} %get-tuple-element.77), channel_id=1, source_target_pairs={{1,0},{2,1},{3,2},{5,4},{6,5},{7,6},{9,8},{10,9},{11,10},{13,12},{... | collective-permute-start | bytes 49160 | tf_op jit(solution)/shard_map/ppermute | solution.py:24
  219.2 19.2 %copy-start.2 = (f32[16,32,128]{2,1,0:T(8,128)}, f32[16,32,128]{2,1,0:T(8,128)S(1)}, u32[]{:S(2)}) copy-start(f32[16,32,128]{2,1,0:T(8,128)S(1)} %get-tuple-element.54) | copy-start | bytes 786436
  232.0 2.7 collective-permute-start.28
  233.4 4.9 %collective-permute-start.27 = (f32[1,32,128]{2,1,0:T(8,128)S(1)}, f32[1,32,128]{2,1,0:T(8,128)S(1)}, u32[]{:S(2)}, u32[]{:S(2)}) collective-permute-start(f32[1,32,128]{2,1,0:T(8,128)S(1)} %get-tuple-element.75), channel_id=1, source_target_pairs={{1,0},{2,1},{3,2},{5,4},{6,5},{7,6},{9,8},{10,9},{11,10},{13,12},{... | collective-permute-start | bytes 49160 | tf_op jit(solution)/shard_map/ppermute | solution.py:24
  253.9 2.7 collective-permute-start.30
  255.3 4.9 %collective-permute-start.29 = (f32[1,32,128]{2,1,0:T(8,128)S(1)}, f32[1,32,128]{2,1,0:T(8,128)S(1)}, u32[]{:S(2)}, u32[]{:S(2)}) collective-permute-start(f32[1,32,128]{2,1,0:T(8,128)S(1)} %get-tuple-element.73), channel_id=1, source_target_pairs={{1,0},{2,1},{3,2},{5,4},{6,5},{7,6},{9,8},{10,9},{11,10},{13,12},{... | collective-permute-start | bytes 49160 | tf_op jit(solution)/shard_map/ppermute | solution.py:24
where the time goes:
time: 277 us; the launch traced here: 275 us
  blocking collectives  105 us (38%)
  starting transfers between devices  52.4 us (19%)
  waiting for transfers between devices  47.4 us (17%)
  between operations  43.6 us (16%)
  other arithmetic  26.7 us (10%)
    psum x12, blocking collectives, pair_sums(): lax.psum((jnp.sum(residual * residual), jnp.sum(residual * applied)), 'sp...  105 us
    ppermute x15, waiting for transfers between devices, extended(): lax.ppermute(head, axis, [((i + 1) % count, i) for i in range(ends)])  45.1 us
    ppermute x15, starting transfers between devices, extended(): lax.ppermute(tail, axis, [(i, (i + 1) % count) for i in range(ends)])  27.7 us
    ppermute x15, starting transfers between devices, extended(): lax.ppermute(head, axis, [((i + 1) % count, i) for i in range(ends)])  19.8 us
    reduce_sum x12, other arithmetic, pair_sums(): jnp.sum(residual * applied)  14.9 us
  transfers between devices with their start and end apart: 31, of which 15 were waited for; matrix products, arithmetic and copies ran while one was open for 1% of the time, Pallas kernels for 0%

commit v1 on v0

v1 whole, which is shorter than its diff:
```python
import functools

import jax
import jax.numpy as jnp
from jax import lax
from jax.experimental import pallas as pl
from jax.experimental.pallas import tpu as pltpu
from jax.sharding import PartitionSpec as P

ITERS = 6
STEPS = 2
STEP_RATE = 4.0
SOURCE_WEIGHT = 0.25
HALO = ITERS * STEPS + 1
OFF = HALO + 1
SUB = 8


def kernel(nt, ns, depth, rows, c_hbm, corr_hbm, cond_hbm, f_hbm, out_hbm,
           c_nat, g_nat, k_nat, f_nat, out_nat, x_buf, r_buf, w_buf, p_buf, q_buf, d_buf,
           dg, cx, cy, cz, slots, totals,
           in_sem, out_sem, corr_send, corr_recv, halo_send, halo_recv, red_send, red_recv):
    tm = lax.axis_index("tm")
    me = lax.axis_index("space")
    jn = rows // SUB
    top = OFF + depth
    planes = top + OFF
    half = 0.5 * STEP_RATE

    loads = [
        pltpu.make_async_copy(cond_hbm, k_nat.at[pl.ds(OFF, depth)], in_sem.at[0]),
        pltpu.make_async_copy(c_hbm.at[0], c_nat, in_sem.at[1]),
        pltpu.make_async_copy(f_hbm, f_nat.at[pl.ds(OFF, depth)], in_sem.at[2]),
    ]
    for load in loads:
        load.start()

    barrier = pltpu.get_barrier_semaphore()
    for other in range(1, ns):
        pl.semaphore_signal(barrier, inc=1, device_id={"space": lax.rem(me + other, ns)})

    @pl.when(tm > 0)
    def _():
        pl.semaphore_signal(barrier, inc=1, device_id={"tm": tm - 1})

    pl.semaphore_wait(barrier, ns - 1 + jnp.where(tm < nt - 1, 1, 0))

    corr = pltpu.make_async_remote_copy(
        src_ref=corr_hbm.at[0], dst_ref=g_nat, send_sem=corr_send, recv_sem=corr_recv,
        device_id={"tm": jnp.minimum(tm + 1, nt - 1)})

    @pl.when(tm < nt - 1)
    def _():
        corr.start()

    def halo(src, src_off, dst, width, slot):
        up = pltpu.make_async_remote_copy(
            src_ref=src.at[pl.ds(src_off + depth - width, width)],
            dst_ref=dst.at[pl.ds(OFF - width, width)],
            send_sem=halo_send.at[2 * slot], recv_sem=halo_recv.at[2 * slot],
            device_id={"space": jnp.minimum(me + 1, ns - 1)})
        down = pltpu.make_async_remote_copy(
            src_ref=src.at[pl.ds(src_off, width)],
            dst_ref=dst.at[pl.ds(top, width)],
            send_sem=halo_send.at[2 * slot + 1], recv_sem=halo_recv.at[2 * slot + 1],
            device_id={"space": jnp.maximum(me - 1, 0)})

        def start():
            pl.when(me < ns - 1)(up.start)
            pl.when(me > 0)(down.start)

        def wait():
            pl.when(me > 0)(up.wait_recv)
            pl.when(me < ns - 1)(down.wait_recv)

        def wait_send():
            pl.when(me < ns - 1)(up.wait_send)
            pl.when(me > 0)(down.wait_send)

        return start, wait, wait_send

    k_halo = halo(cond_hbm, 0, k_nat, HALO, 0)
    f_halo = halo(f_hbm, 0, f_nat, HALO - 1, 1)
    x_halo = halo(x_buf, OFF, x_buf, HALO, 2)
    k_halo[0]()
    f_halo[0]()

    zero_plane = jnp.zeros((rows, 128), jnp.float32)
    zero_tiles = jnp.zeros((jn, SUB, 128), jnp.float32)

    def clear(lo, count):
        def one(i, carry):
            k_nat[lo + i] = zero_plane
            f_nat[lo + i] = zero_plane
            x_buf[lo + i] = zero_tiles
            return carry
        lax.fori_loop(0, count, one, 0)

    clear(0, 1)
    clear(planes - 1, 1)
    pl.when(me == 0)(lambda: clear(1, HALO))
    pl.when(me == ns - 1)(lambda: clear(top, HALO))

    for buf in (r_buf, d_buf):
        buf[0] = zero_tiles
        buf[1] = zero_tiles
        buf[planes - 2] = zero_tiles
        buf[planes - 1] = zero_tiles

    lane = lax.broadcasted_iota(jnp.int32, (SUB, 128), 1)
    sub = lax.broadcasted_iota(jnp.int32, (SUB, 128), 0)
    inner_lane = jnp.where(lane < 127, 1.0, 0.0)
    first_lane = jnp.where(lane > 0, 1.0, 0.0)
    inner_sub = jnp.where(sub < SUB - 1, 1.0, 0.0)
    first_sub = jnp.where(sub > 0, 1.0, 0.0)

    def nat(ref, p, j):
        return ref[p, pl.ds(j, SUB, stride=jn), :]

    def ahead(x):
        return pltpu.roll(x, 127, 1)

    def behind(x):
        return pltpu.roll(x, 1, 1)

    def sub_ahead(x):
        return pltpu.roll(x, SUB - 1, 0)

    def sub_behind(x):
        return pltpu.roll(x, 1, 0)

    loads[0].wait()
    k_halo[1]()

    def make_weights(i, carry):
        p = i + 1
        k = [nat(k_nat, p, j) for j in range(jn)]
        up = [nat(k_nat, p + 1, j) for j in range(jn)]
        dn = [nat(k_nat, p - 1, j) for j in range(jn)]
        z = me * depth + p - OFF
        face = jnp.where((z >= 0) & (z + 1 < ns * depth), -half, 0.0)
        for j in range(jn):
            right = ahead(k[j]) * inner_lane
            left = behind(k[j]) * first_lane
            yp = k[j + 1] if j + 1 < jn else sub_ahead(k[0]) * inner_sub
            ym = k[j - 1] if j > 0 else sub_behind(k[jn - 1]) * first_sub
            around = right + left + yp + ym + up[j] + dn[j]
            dg[p, j] = 1.0 + half * (6.0 * k[j] + around)
            cx[p, j] = -half * (k[j] + right) * inner_lane
            wy = -half * (k[j] + yp)
            cy[p, j] = wy if j + 1 < jn else wy * inner_sub
            cz[p, j] = face * (k[j] + up[j])
        return carry

    lax.fori_loop(0, planes - 2, make_weights, 0)

    def apply(ref, p):
        v = [ref[p, j] for j in range(jn)]
        c = [cx[p, j] for j in range(jn)]
        y = [cy[p, j] for j in range(jn)]
        rolled = [ahead(v[j]) for j in range(jn)]
        back = [behind(c[j] * v[j]) for j in range(jn)]
        out = []
        for j in range(jn):
            acc = dg[p, j] * v[j] + cz[p, j] * ref[p + 1, j] + cz[p - 1, j] * ref[p - 1, j]
            acc = acc + y[j] * (v[j + 1] if j + 1 < jn else sub_ahead(v[0]))
            acc = acc + (y[j - 1] * v[j - 1] if j > 0 else sub_behind(y[jn - 1] * v[jn - 1]))
            out.append(acc + (c[j] * rolled[j] + back[j]))
        return out, v

    def both_halos(width, fn):
        count = (width + 1) // 2

        def step(i, carry):
            for t in range(2):
                fn(OFF - 1 - (2 * i + t))
                fn(top + 2 * i + t)
            return carry
        if count:
            lax.fori_loop(0, count, step, 0)

    def own(fn, carry, chunk=4):
        def step(i, carry):
            for t in range(chunk):
                carry = fn(OFF + i * chunk + t, carry)
            return carry
        return lax.fori_loop(0, depth // chunk, step, carry)

    loads[1].wait()

    @pl.when(tm > 0)
    def _():
        corr.wait_recv()

        def add(p, carry):
            for j in range(jn):
                x_buf[p, j] = nat(c_nat, p - OFF, j) + nat(g_nat, p - OFF, j)
            return carry
        own(add, 0)

    @pl.when(tm == 0)
    def _():
        def add(p, carry):
            for j in range(jn):
                x_buf[p, j] = nat(c_nat, p - OFF, j)
            return carry
        own(add, 0)

    x_halo[0]()
    loads[2].wait()
    f_halo[1]()

    def first_residual(p):
        image, v = apply(x_buf, p)
        for j in range(jn):
            r_buf[p, j] = (v[j] + SOURCE_WEIGHT * nat(f_nat, p, j)) - image[j]

    def first_own(i, carry):
        for t in range(2):
            first_residual(OFF + 1 + 2 * i + t)
        return carry

    lax.fori_loop(0, (depth - 2) // 2, first_own, 0)
    x_halo[1]()
    x_halo[2]()
    first_residual(OFF)
    first_residual(top - 1)
    both_halos(HALO - 1, first_residual)

    def spread(row):
        return jnp.broadcast_to(row, (SUB, 128))

    def reduce(stage, parts):
        for i, part in enumerate(parts):
            slots[stage, me, i:i + 1] = jnp.sum(part, axis=0, keepdims=True)
        for i in range(len(parts), SUB):
            slots[stage, me, i:i + 1] = jnp.zeros((1, 128), jnp.float32)
        copies = []
        for other in range(1, ns):
            copies.append(pltpu.make_async_remote_copy(
                src_ref=slots.at[stage, me], dst_ref=slots.at[stage, me],
                send_sem=red_send.at[stage, other], recv_sem=red_recv.at[stage, other],
                device_id={"space": lax.rem(me + other, ns)}))
        for copy in copies:
            copy.start()
        for copy in copies:
            copy.wait()
        total = slots[stage, 0]
        for i in range(1, ns):
            total = total + slots[stage, i]
        totals[stage] = jnp.broadcast_to(jnp.sum(total, axis=1, keepdims=True), (SUB, 128))
        return [spread(totals[stage, i:i + 1]) for i in range(len(parts))]

    zero = jnp.zeros((SUB, 128), jnp.float32)
    for section in range(STEPS):
        for sweep in range(ITERS):
            n = section * ITERS + sweep
            width = HALO - 2 - n

            def image_at(p):
                image, v = apply(r_buf, p)
                for j in range(jn):
                    w_buf[p, j] = image[j]
                return image, v

            def image_own(p, carry):
                rr, rw = carry
                image, v = image_at(p)
                for j in range(jn):
                    rr = rr + v[j] * v[j]
                    rw = rw + v[j] * image[j]
                return rr, rw

            rr, rw = reduce_in = own(image_own, (zero, zero))
            both_halos(width, image_at)
            norm, product = reduce(n, reduce_in)
            if sweep == 0:
                step_length = norm / product
                beta = None
            else:
                beta = norm / norm_before
                step_length = norm / (product - beta * norm / step_length)
            norm_before = norm
            last_sweep = sweep + 1 == ITERS
            last = last_sweep and section + 1 == STEPS

            def update(p, is_own):
                for j in range(jn):
                    r = r_buf[p, j]
                    pp = r if beta is None else r + beta * p_buf[p, j]
                    d = step_length * pp
                    if beta is not None:
                        d = d_buf[p, j] + d
                    if not last_sweep:
                        p_buf[p, j] = pp
                    if not last:
                        w = w_buf[p, j]
                        q = w if beta is None else w + beta * q_buf[p, j]
                        r = r - step_length * q
                        if last_sweep:
                            r = r + d
                        else:
                            q_buf[p, j] = q
                        r_buf[p, j] = r
                    if last_sweep:
                        if is_own:
                            x = x_buf[p, j] + d
                            if not last:
                                x_buf[p, j] = x
                            out_nat[section, p - OFF, pl.ds(j, SUB, stride=jn), :] = x
                    else:
                        d_buf[p, j] = d

            def update_own(p, carry):
                update(p, True)
                return carry

            own(update_own, 0)
            if not last:
                both_halos(width, lambda p: update(p, False))
        pltpu.make_async_copy(out_nat.at[section], out_hbm.at[0, section], out_sem.at[section]).start()

    for section in range(STEPS):
        pltpu.make_async_copy(out_nat.at[section], out_hbm.at[0, section], out_sem.at[section]).wait()
    k_halo[2]()
    f_halo[2]()

    @pl.when(tm < nt - 1)
    def _():
        corr.wait_send()


def solution(mesh):
    nt, ns = mesh.shape["tm"], mesh.shape["space"]

    def body(c_points, corrections, conductivity, forcing):
        depth, rows, lanes = conductivity.shape
        planes = depth + 2 * OFF
        jn = rows // SUB
        nat = pltpu.VMEM((depth, rows, lanes), jnp.float32)
        wide = pltpu.VMEM((planes, rows, lanes), jnp.float32)
        tiles = pltpu.VMEM((planes, jn, SUB, lanes), jnp.float32)
        dma = pltpu.SemaphoreType.DMA
        stages = STEPS * ITERS
        return pl.pallas_call(
            functools.partial(kernel, nt, ns, depth, rows),
            out_shape=jax.ShapeDtypeStruct((1, STEPS, depth, rows, lanes), jnp.float32),
            in_specs=[pl.BlockSpec(memory_space=pl.ANY)] * 4,
            out_specs=pl.BlockSpec(memory_space=pl.ANY),
            scratch_shapes=[
                nat, nat, wide, wide,
                pltpu.VMEM((STEPS, depth, rows, lanes), jnp.float32),
                tiles, tiles, tiles, tiles, tiles, tiles,
                tiles, tiles, tiles, tiles,
                pltpu.VMEM((stages, ns, SUB, lanes), jnp.float32),
                pltpu.VMEM((stages, SUB, lanes), jnp.float32),
                dma((3,)), dma((STEPS,)), dma, dma, dma((6,)), dma((6,)),
                dma((stages, ns)), dma((stages, ns)),
            ],
            compiler_params=pltpu.CompilerParams(
                collective_id=0, has_side_effects=True, vmem_limit_bytes=48 * 1024 * 1024),
        )(c_points, corrections, conductivity, forcing)

    in_specs = (
        P("tm", "space", None, None),
        P("tm", "space", None, None),
        P("space", None, None),
        P("space", None, None),
    )
    out_specs = P("tm", None, "space", None, None)
    return jax.shard_map(body, mesh=mesh, in_specs=in_specs, out_specs=out_specs, check_vma=False)
```

time: 277 us -> 64.8 us (0.23)
  blocking collectives: 105 us -> 0 us
  Pallas kernels: 0 us -> 60 us
  starting transfers between devices: 52.4 us -> 0 us
  waiting for transfers between devices: 47.4 us -> 0 us
  between operations: 43.6 us -> 0.01 us
  other arithmetic: 26.7 us -> 0 us
  local copies, waits for them, and re-layouts: 0.83 us -> 4.59 us
    psum x12 -> x0, blocking collectives: 105 us -> none  [pair_sums(): lax.psum((jnp.sum(residual * residual), jnp.sum(residual * applied)), 'sp...]
    pallas_call x0 -> x1, Pallas kernels: none -> 60 us  [body(): pl.pallas_call(functools.partial(kernel, nt, ns, depth, rows), out_shape=...]
    ppermute x31 -> x0, starting transfers between devices: 52.4 us -> none  [the longest x15 27.7 us: extended(): lax.ppermute(tail, axis, [(i, (i + 1) % count) for i in range(ends)])]
    ppermute x31 -> x0, waiting for transfers between devices: 47.4 us -> none  [the longest x15 45.1 us: extended(): lax.ppermute(head, axis, [((i + 1) % count, i) for i in range(ends)])]
    reduce_sum x12 -> x0, other arithmetic: 14.9 us -> none  [pair_sums(): jnp.sum(residual * applied)]
    sub x12 -> x0, other arithmetic: 5.64 us -> none  [the longest x10 4.68 us: body(): residual = residual - step_length * along_dir]
    unnamed x10 -> x9, local copies, waits for them, and re-layouts: 0.03 us -> 4.59 us
    concatenate x15 -> x0, other arithmetic: 3.86 us -> none  [extended(): jnp.concatenate([lax.ppermute(tail, axis, [(i, (i + 1) % count) for i in...]
  transfers between devices with their start and end apart: 31 -> 0, of which waited for: 15 -> 0; matrix products, arithmetic and copies ran while one was open for 1% -> 0% of each run, Pallas kernels for 0% -> 0%
where the time goes in v1:
time: 64.8 us; the launch traced here: 64.6 us
  Pallas kernels  60 us (93%)
  local copies, waits for them, and re-layouts  4.59 us (7%)
    pallas_call x1, Pallas kernels, body(): pl.pallas_call(functools.partial(kernel, nt, ns, depth, rows), out_shape=...  60 us
    unnamed x9, local copies, waits for them, and re-layouts  4.59 us

profile of v1, /device:TPU:0, one launch (start us, length us, event | category | flops | bytes accessed | tf_op | source)
XLA Modules:
  0.0 64.6 jit_solution(11042794392846931403)
XLA Ops:
  0.0 0.0 copy-start
  0.0 0.9 %copy-done = f32[1,16,32,128]{3,2,1,0:T(8,128)S(1)} copy-done((f32[1,16,32,128]{3,2,1,0:T(8,128)S(1)}, f32[1,16,32,128]{3,2,1,0:T(8,128)}, u32[]{:S(2)}) %copy-start) | copy-done | bytes 262168
  1.0 0.0 copy-start.1
  1.0 0.9 %copy-done.1 = f32[1,16,32,128]{3,2,1,0:T(8,128)S(1)} copy-done((f32[1,16,32,128]{3,2,1,0:T(8,128)S(1)}, f32[1,16,32,128]{3,2,1,0:T(8,128)}, u32[]{:S(2)}) %copy-start.1) | copy-done | bytes 262168
  1.9 0.0 copy-start.2
  1.9 0.9 %copy-done.2 = f32[16,32,128]{2,1,0:T(8,128)S(1)} copy-done((f32[16,32,128]{2,1,0:T(8,128)S(1)}, f32[16,32,128]{2,1,0:T(8,128)}, u32[]{:S(2)}) %copy-start.2) | copy-done | bytes 262168
  2.9 0.0 copy-start.3
  2.9 0.9 %copy-done.3 = f32[16,32,128]{2,1,0:T(8,128)S(1)} copy-done((f32[16,32,128]{2,1,0:T(8,128)S(1)}, f32[16,32,128]{2,1,0:T(8,128)}, u32[]{:S(2)}) %copy-start.3) | copy-done | bytes 262168
  3.8 60.0 %shard_map.46 = f32[1,2,16,32,128]{4,3,2,1,0:T(8,128)S(1)} custom-call(f32[1,16,32,128]{3,2,1,0:T(8,128)S(1)} %copy-done, f32[1,16,32,128]{3,2,1,0:T(8,128)S(1)} %copy-done.1, f32[16,32,128]{2,1,0:T(8,128)S(1)} %copy-done.2, f32[16,32,128]{2,1,0:T(8,128)S(1)} %copy-done.3), custom_call_target="tpu_custom_call" | custom-call | tf_op jit(solution)/shard_map/pallas_call | solution.py:345
  63.8 0.8 %copy.6 = f32[1,2,16,32,128]{4,3,2,1,0:T(8,128)} copy(f32[1,2,16,32,128]{4,3,2,1,0:T(8,128)S(1)} %shard_map.46) | data formatting | bytes 1048576
Async XLA Ops:
  0.0 0.9 %copy-start = (f32[1,16,32,128]{3,2,1,0:T(8,128)S(1)}, f32[1,16,32,128]{3,2,1,0:T(8,128)}, u32[]{:S(2)}) copy-start(f32[1,16,32,128]{3,2,1,0:T(8,128)} %c_hbm.1) | copy-start | bytes 786436
  1.0 0.9 %copy-start.1 = (f32[1,16,32,128]{3,2,1,0:T(8,128)S(1)}, f32[1,16,32,128]{3,2,1,0:T(8,128)}, u32[]{:S(2)}) copy-start(f32[1,16,32,128]{3,2,1,0:T(8,128)} %corr_hbm.1) | copy-start | bytes 786436
  1.9 0.9 %copy-start.2 = (f32[16,32,128]{2,1,0:T(8,128)S(1)}, f32[16,32,128]{2,1,0:T(8,128)}, u32[]{:S(2)}) copy-start(f32[16,32,128]{2,1,0:T(8,128)} %cond_hbm.1) | copy-start | bytes 786436
  2.9 0.9 %copy-start.3 = (f32[16,32,128]{2,1,0:T(8,128)S(1)}, f32[16,32,128]{2,1,0:T(8,128)}, u32[]{:S(2)}) copy-start(f32[16,32,128]{2,1,0:T(8,128)} %f_hbm.1) | copy-start | bytes 786436

commit v2 on v1

--- a/solution.py
+++ b/solution.py
@@ -17,7 +17,7 @@
 
 
 def kernel(nt, ns, depth, rows, c_hbm, corr_hbm, cond_hbm, f_hbm, out_hbm,
-           c_nat, g_nat, k_nat, f_nat, out_nat, x_buf, r_buf, w_buf, p_buf, q_buf, d_buf,
+           c_nat, g_nat, k_nat, f_nat, out_nat, x_buf, r_buf, w_buf, p_buf, q_buf, d_buf, t_buf, o_buf,
            dg, cx, cy, cz, slots, totals,
            in_sem, out_sem, corr_send, corr_recv, halo_send, halo_recv, red_send, red_recv):
     tm = lax.axis_index("tm")
@@ -101,7 +101,7 @@
     pl.when(me == 0)(lambda: clear(1, HALO))
     pl.when(me == ns - 1)(lambda: clear(top, HALO))
 
-    for buf in (r_buf, d_buf):
+    for buf in (r_buf, w_buf):
         buf[0] = zero_tiles
         buf[1] = zero_tiles
         buf[planes - 2] = zero_tiles
@@ -253,63 +253,96 @@
 
     zero = jnp.zeros((SUB, 128), jnp.float32)
     for section in range(STEPS):
-        for sweep in range(ITERS):
-            n = section * ITERS + sweep
-            width = HALO - 2 - n
+        for pair in range(ITERS // 2):
+            n = section * (ITERS // 2) + pair
+            width = HALO - 3 - 2 * n
+            fresh = pair == 0
 
             def image_at(p):
-                image, v = apply(r_buf, p)
+                image, _ = apply(r_buf, p)
                 for j in range(jn):
                     w_buf[p, j] = image[j]
+
+            def image_own(p, carry):
+                image_at(p)
+                return carry
+
+            own(image_own, 0)
+            both_halos(width + 1, image_at)
+
+            def twice_at(p):
+                image, v = apply(w_buf, p)
+                for j in range(jn):
+                    t_buf[p, j] = image[j]
                 return image, v
 
-            def image_own(p, carry):
-                rr, rw = carry
-                image, v = image_at(p)
+            def twice_own(p, sums):
+                t, w = twice_at(p)
+                sums = list(sums)
                 for j in range(jn):
-                    rr = rr + v[j] * v[j]
-                    rw = rw + v[j] * image[j]
-                return rr, rw
-
-            rr, rw = reduce_in = own(image_own, (zero, zero))
-            both_halos(width, image_at)
-            norm, product = reduce(n, reduce_in)
-            if sweep == 0:
-                step_length = norm / product
+                    r = r_buf[p, j]
+                    terms = [r * r, r * w[j], w[j] * w[j], w[j] * t[j]]
+                    if not fresh:
+                        q = q_buf[p, j]
+                        z = (o_buf[p, j] - w[j]) * inverse
+                        terms += [w[j] * q, q * q, t[j] * q, q * z]
+                    sums = [total + term for total, term in zip(sums, terms)]
+                return tuple(sums)
+
+            sums = own(twice_own, (zero,) * (4 if fresh else 8))
+            both_halos(width, twice_at)
+            dots = reduce(n, sums)
+            rr, rw, ww, wt = dots[:4]
+            if fresh:
                 beta = None
+                alpha = rr / rw
+                wq, qq, qz = ww, ww, wt
             else:
-                beta = norm / norm_before
-                step_length = norm / (product - beta * norm / step_length)
+                wq_old, qq_old, tq_old, qz_old = dots[4:]
+                beta = rr / norm_before
+                alpha = rr / (rw - beta * rr * inverse)
+                wq = ww + beta * wq_old
+                qq = wq + beta * (wq_old + beta * qq_old)
+                qz = wt + beta * (2.0 * tq_old + beta * qz_old)
+            norm = alpha * alpha * qq - rr
+            beta_next = norm / rr
+            along = rw + alpha * (alpha * qz - 2.0 * wq)
+            alpha_next = norm / (along - beta_next * norm / alpha)
+            inverse_before = None if fresh else inverse
+            inverse = 1.0 / alpha_next
             norm_before = norm
-            last_sweep = sweep + 1 == ITERS
-            last = last_sweep and section + 1 == STEPS
+            last_pair = pair + 1 == ITERS // 2
+            last = last_pair and section + 1 == STEPS
 
             def update(p, is_own):
                 for j in range(jn):
-                    r = r_buf[p, j]
-                    pp = r if beta is None else r + beta * p_buf[p, j]
-                    d = step_length * pp
-                    if beta is not None:
+                    r, w, t = r_buf[p, j], w_buf[p, j], t_buf[p, j]
+                    if fresh:
+                        pp, q, z = r, w, t
+                    else:
+                        pp = r + beta * p_buf[p, j]
+                        q = w + beta * q_buf[p, j]
+                        z = t + beta * ((o_buf[p, j] - w) * inverse_before)
+                    r = r - alpha * q
+                    p_next = r + beta_next * pp
+                    d = alpha * pp + alpha_next * p_next
+                    if not fresh:
                         d = d_buf[p, j] + d
-                    if not last_sweep:
-                        p_buf[p, j] = pp
                     if not last:
-                        w = w_buf[p, j]
-                        q = w if beta is None else w + beta * q_buf[p, j]
-                        r = r - step_length * q
-                        if last_sweep:
-                            r = r + d
-                        else:
-                            q_buf[p, j] = q
-                        r_buf[p, j] = r
-                    if last_sweep:
-                        if is_own:
-                            x = x_buf[p, j] + d
-                            if not last:
-                                x_buf[p, j] = x
-                            out_nat[section, p - OFF, pl.ds(j, SUB, stride=jn), :] = x
-                    else:
+                        w = w - alpha * z
+                        q = w + beta_next * q
+                        r = r - alpha_next * q
+                        r_buf[p, j] = r + d if last_pair else r
+                    if not last_pair:
+                        p_buf[p, j] = p_next
+                        q_buf[p, j] = q
+                        o_buf[p, j] = w
                         d_buf[p, j] = d
+                    elif is_own:
+                        x = x_buf[p, j] + d
+                        if not last:
+                            x_buf[p, j] = x
+                        out_nat[section, p - OFF, pl.ds(j, SUB, stride=jn), :] = x
 
             def update_own(p, carry):
                 update(p, True)
@@ -341,7 +374,7 @@
         wide = pltpu.VMEM((planes, rows, lanes), jnp.float32)
         tiles = pltpu.VMEM((planes, jn, SUB, lanes), jnp.float32)
         dma = pltpu.SemaphoreType.DMA
-        stages = STEPS * ITERS
+        stages = STEPS * (ITERS // 2)
         return pl.pallas_call(
             functools.partial(kernel, nt, ns, depth, rows),
             out_shape=jax.ShapeDtypeStruct((1, STEPS, depth, rows, lanes), jnp.float32),
@@ -350,7 +383,7 @@
             scratch_shapes=[
                 nat, nat, wide, wide,
                 pltpu.VMEM((STEPS, depth, rows, lanes), jnp.float32),
-                tiles, tiles, tiles, tiles, tiles, tiles,
+                tiles, tiles, tiles, tiles, tiles, tiles, tiles, tiles,
                 tiles, tiles, tiles, tiles,
                 pltpu.VMEM((stages, ns, SUB, lanes), jnp.float32),
                 pltpu.VMEM((stages, SUB, lanes), jnp.float32),

time: 64.8 us -> 47.9 us (0.74)
  Pallas kernels: 60 us -> 43.1 us
    pallas_call x1, Pallas kernels: 60 us -> 43.1 us  [body(): pl.pallas_call(functools.partial(kernel, nt, ns, depth, rows), out_shape=...]
where the time goes in v2:
time: 47.9 us; the launch traced here: 47.7 us
  Pallas kernels  43.1 us (90%)
  local copies, waits for them, and re-layouts  4.59 us (10%)
    pallas_call x1, Pallas kernels, body(): pl.pallas_call(functools.partial(kernel, nt, ns, depth, rows), out_shape=...  43.1 us
    unnamed x9, local copies, waits for them, and re-layouts  4.59 us

profile of v2, /device:TPU:0, one launch (start us, length us, event | category | flops | bytes accessed | tf_op | source)
XLA Modules:
  0.0 47.7 jit_solution(12786765406544726497)
XLA Ops:
  0.0 0.0 copy-start
  0.0 0.9 %copy-done = f32[1,16,32,128]{3,2,1,0:T(8,128)S(1)} copy-done((f32[1,16,32,128]{3,2,1,0:T(8,128)S(1)}, f32[1,16,32,128]{3,2,1,0:T(8,128)}, u32[]{:S(2)}) %copy-start) | copy-done | bytes 262168
  1.0 0.0 copy-start.1
  1.0 0.9 %copy-done.1 = f32[1,16,32,128]{3,2,1,0:T(8,128)S(1)} copy-done((f32[1,16,32,128]{3,2,1,0:T(8,128)S(1)}, f32[1,16,32,128]{3,2,1,0:T(8,128)}, u32[]{:S(2)}) %copy-start.1) | copy-done | bytes 262168
  1.9 0.0 copy-start.2
  1.9 0.9 %copy-done.2 = f32[16,32,128]{2,1,0:T(8,128)S(1)} copy-done((f32[16,32,128]{2,1,0:T(8,128)S(1)}, f32[16,32,128]{2,1,0:T(8,128)}, u32[]{:S(2)}) %copy-start.2) | copy-done | bytes 262168
  2.9 0.0 copy-start.3
  2.9 0.9 %copy-done.3 = f32[16,32,128]{2,1,0:T(8,128)S(1)} copy-done((f32[16,32,128]{2,1,0:T(8,128)S(1)}, f32[16,32,128]{2,1,0:T(8,128)}, u32[]{:S(2)}) %copy-start.3) | copy-done | bytes 262168
  3.8 43.1 %shard_map.46 = f32[1,2,16,32,128]{4,3,2,1,0:T(8,128)S(1)} custom-call(f32[1,16,32,128]{3,2,1,0:T(8,128)S(1)} %copy-done, f32[1,16,32,128]{3,2,1,0:T(8,128)S(1)} %copy-done.1, f32[16,32,128]{2,1,0:T(8,128)S(1)} %copy-done.2, f32[16,32,128]{2,1,0:T(8,128)S(1)} %copy-done.3), custom_call_target="tpu_custom_call" | custom-call | tf_op jit(solution)/shard_map/pallas_call | solution.py:378
  46.9 0.8 %copy.6 = f32[1,2,16,32,128]{4,3,2,1,0:T(8,128)} copy(f32[1,2,16,32,128]{4,3,2,1,0:T(8,128)S(1)} %shard_map.46) | data formatting | bytes 1048576
Async XLA Ops:
  0.0 0.9 %copy-start = (f32[1,16,32,128]{3,2,1,0:T(8,128)S(1)}, f32[1,16,32,128]{3,2,1,0:T(8,128)}, u32[]{:S(2)}) copy-start(f32[1,16,32,128]{3,2,1,0:T(8,128)} %c_hbm.1) | copy-start | bytes 786436
  1.0 0.9 %copy-start.1 = (f32[1,16,32,128]{3,2,1,0:T(8,128)S(1)}, f32[1,16,32,128]{3,2,1,0:T(8,128)}, u32[]{:S(2)}) copy-start(f32[1,16,32,128]{3,2,1,0:T(8,128)} %corr_hbm.1) | copy-start | bytes 786436
  1.9 0.9 %copy-start.2 = (f32[16,32,128]{2,1,0:T(8,128)S(1)}, f32[16,32,128]{2,1,0:T(8,128)}, u32[]{:S(2)}) copy-start(f32[16,32,128]{2,1,0:T(8,128)} %cond_hbm.1) | copy-start | bytes 786436
  2.9 0.9 %copy-start.3 = (f32[16,32,128]{2,1,0:T(8,128)S(1)}, f32[16,32,128]{2,1,0:T(8,128)}, u32[]{:S(2)}) copy-start(f32[16,32,128]{2,1,0:T(8,128)} %f_hbm.1) | copy-start | bytes 786436
